TPU v7x, 512 devices: a whole 4x8x8 slice. The times are simulated.
512 devices in a mesh: fsdp: 64 (over x, y, core), dp: 8 (over z).
Axes of the slice: x: 4, y: 8, z: 8, core: 2. Of those that a mesh axis runs over, the one named last changes fastest.
Arguments:
- grads: bfloat16 [8, 1024, 28672], P('dp', 'fsdp')
- block_slot: int32 [28], replicated, may hold values from 0 to 63, as said below
- left_stats: float32 [64, 1024, 1024], P('fsdp', 'dp')
- right_stats: float32 [64, 1024, 1024], P('fsdp', 'dp')
- left_root: bfloat16 [64, 1024, 1024], P('fsdp', 'dp')
- right_root: bfloat16 [64, 1024, 1024], P('fsdp', 'dp')
Outputs:
- left_new: float32 [64, 1024, 1024], P('fsdp', 'dp')
- right_new: float32 [64, 1024, 1024], P('fsdp', 'dp')
- update: bfloat16 [1024, 28672], P('fsdp')
Inputs may be any that keep to these rules, and one draw needn't show every extreme that they name: The entries of block_slot are distinct. Block b's statistics and roots sit in slot block_slot[b], which belongs to the fsdp device of index block_slot[b]; slots that no block names are empty and their statistics pass through unchanged.
All inputs are finite; a program needn't handle non-finite values.
Results may differ from a plain program's by a relative error of at most 0.015.
Values may be sent and summed in bfloat16 or wider, within the bound.
No kernel may reach another device: no remote copies, remote signals or barrier semaphores. Data moves between devices by JAX's collectives and lax.ppermute only.
A program may use at most 64 MiB of HBM per device.

v0:
```python
import jax
import jax.numpy as jnp
from jax import lax
from jax.sharding import Mesh
from jax.sharding import PartitionSpec as P

FSDP = ("fsdp_0", "fsdp_1", "fsdp_2")
epsilon = 1e-06


def in_blocks(array, dim, count):
    lengths = array.shape
    tiles = array.reshape(*lengths[:dim], count, lengths[dim] // count, *lengths[dim + 1 :])
    return jnp.moveaxis(tiles, dim, 0)


def sum_at_owner(array, axis, dim):
    count = lax.axis_size(axis)
    tiles = lax.all_to_all(in_blocks(array, dim, count), axis, 0, 0, tiled=True)
    return jnp.sum(tiles.astype(jnp.float32), axis=0)


def in_order(tiles, dim):
    tiles = jnp.moveaxis(tiles, 0, dim)
    lengths = tiles.shape
    return tiles.reshape(*lengths[:dim], lengths[dim] * lengths[dim + 1], *lengths[dim + 2 :])


def exchange_in_order(tiles, axes, sequence):
    inside = tiles.shape[1:]
    result = tiles.reshape(*(lax.axis_size(a) for a in axes), *inside)
    for k in sequence:
        result = lax.all_to_all(result, axes[k], k, k, tiled=True)
    return result.reshape(-1, *inside)


def core_and_chips(array, groups, sequence, split_dim, concat_dim):
    count = lax.axis_size(groups[0]) * lax.axis_size(groups[1])
    tiles = in_blocks(array, split_dim, count)
    return in_order(exchange_in_order(tiles, groups, sequence), concat_dim)


def per_device(grads, block_slot, left_stats, right_stats, left_root, right_root):
    local_rows = grads[0]
    row_dev, col_count = local_rows.shape
    block_size = left_stats.shape[2]
    block_count = col_count // block_size
    slot_count = left_stats.shape[0]
    shared_rows = left_stats.shape[1]
    total_slots = slot_count * lax.axis_size(FSDP)
    slot_ids = jnp.arange(total_slots, dtype=jnp.int32)
    matches = block_slot[None, :] == slot_ids[:, None]
    filled = jnp.any(matches, axis=1)
    source = jnp.sum(
        jnp.where(matches, jnp.arange(block_count, dtype=jnp.int32)[None, :], 0), axis=1
    )
    row_start = lax.axis_index("dp") * shared_rows
    band = local_rows.astype(jnp.float32).reshape(row_dev, block_count, block_size)
    shares = sum_at_owner(band.astype(jnp.bfloat16), "dp", 2).astype(jnp.bfloat16)
    outgoing = jnp.where(
        filled[None, :, None], jnp.take(shares, source, axis=1), jnp.zeros((), jnp.bfloat16)
    )
    incoming = lax.all_to_all(outgoing, FSDP, split_axis=1, concat_axis=0, tiled=True)
    gradient = lax.all_gather(incoming, "dp", axis=2, tiled=True)
    own_rows = lax.dynamic_slice_in_dim(gradient, row_start, shared_rows, 0)
    whole_right = lax.all_gather(right_root, "dp", axis=1, tiled=True)
    left_new = left_stats + jnp.einsum(
        "rjc,kjc->jrk", own_rows, gradient, preferred_element_type=jnp.float32
    )
    columns = lax.dynamic_slice_in_dim(gradient, row_start, shared_rows, 2)
    right_new = right_stats + jnp.einsum(
        "rjc,rjk->jck", columns, gradient, preferred_element_type=jnp.float32
    )
    left_applied = jnp.einsum(
        "jrk,kjc->rjc", left_root, gradient, preferred_element_type=jnp.float32
    ).astype(jnp.bfloat16)
    both_applied = jnp.einsum(
        "rjc,jck->rjk", left_applied, whole_right, preferred_element_type=jnp.float32
    )
    squares = lax.psum(jnp.sum(both_applied * both_applied, axis=(0, 2)), "dp")
    factor = lax.rsqrt(squares / (block_size * block_size) + epsilon)
    scaled = (both_applied * factor[None, :, None]).astype(jnp.bfloat16)
    full_rows = lax.all_gather(scaled, "dp", axis=0, tiled=True)
    returned = core_and_chips(full_rows, (("fsdp_0", "fsdp_1"), "fsdp_2"), (1, 0), 0, 1)
    update = jnp.take(returned, block_slot, axis=1).reshape(row_dev, col_count)
    return (left_new, right_new, update)


def solution(mesh):
    split = Mesh(
        mesh.devices.reshape(4, 8, 2, mesh.shape["dp"]), ("fsdp_0", "fsdp_1", "fsdp_2", "dp")
    )
    placed = (
        P("dp", FSDP, None),
        P(),
        P(FSDP, "dp", None),
        P(FSDP, "dp", None),
        P(FSDP, "dp", None),
        P(FSDP, "dp", None),
    )
    return jax.shard_map(
        per_device,
        mesh=split,
        in_specs=placed,
        out_specs=(P(FSDP, "dp", None), P(FSDP, "dp", None), P(FSDP, None)),
        check_vma=False,
    )
```

profile of v0, /device:TPU:16, one launch (start us, length us, event | category | flops | bytes accessed | tf_op | source)
XLA Modules:
  0.0 264.3 jit_solution(12434636869901836517)
XLA Ops:
  7.2 0.0 all-gather.6.cloned.1.call-start
  7.2 0.7 all-gather.6.cloned.1.call-update
  7.9 1.3 copy.35
  9.2 1.3 copy.27
  10.5 10.3 %all-to-all-start = ((bf16[8,16,28,128]{3,1,2,0:T(8,128)(2,1)}), bf16[8,16,28,128]{3,1,2,0:T(8,128)(2,1)S(1)}, u32[]{:S(2)}, u32[]{:S(2)}) async-start(bf16[8,16,28,128]{3,1,2,0:T(8,128)(2,1)} %copy.27), calls=%async_computation | async-start | bytes 1835008 | tf_op jit(solution)/shard_map/all_to_all | solution.py:19
  20.8 0.0 all-gather.4.cloned.1.call-start
  20.9 0.1 select_reduce_fusion
  21.0 0.1 fusion.35
  21.1 32.4 %all-to-all-done = bf16[8,16,28,128]{3,1,2,0:T(8,128)(2,1)S(1)} async-done(((bf16[8,16,28,128]{3,1,2,0:T(8,128)(2,1)}), bf16[8,16,28,128]{3,1,2,0:T(8,128)(2,1)S(1)}, u32[]{:S(2)}, u32[]{:S(2)}) %all-to-all-start) | async-done | bytes 917536 | tf_op jit(solution)/shard_map/all_to_all | solution.py:19
  53.5 0.1 reduce_sum.35
  53.6 0.6 gather_fusion
  54.2 0.2 select_bitcast_fusion
  54.4 22.2 %all_to_all.33 = bf16[16,64,128]{2,0,1:T(8,128)(2,1)} all-to-all(bf16[16,64,128]{2,0,1:T(8,128)(2,1)S(1)} %select_bitcast_fusion), channel_id=1, replica_groups=mesh['fsdp_0'=4,'fsdp_1'=8,'fsdp_2'=2,'dp'=8] {'fsdp_0','fsdp_1','fsdp_2'}, dimensions={1} | all-to-all | bytes 524288 | tf_op jit(solution)/shard_map/all_to_all | solution.py:63
  76.6 0.0 all-gather.8.cloned.1.call-start
  76.7 0.0 all-gather.6.cloned.1.call-done
  76.7 43.8 %all-gather.4.cloned.1.call-done = bf16[1024,1,1024]{2,0,1:T(8,128)(2,1)} async-done(((bf16[1024,1,128]{2,0,1:T(8,128)(2,1)}), bf16[1024,1,1024]{2,0,1:T(8,128)(2,1)}) %all-gather.4.cloned.1.call-update) | async-done | bytes 2097168 | tf_op jit(solution)/shard_map/all_gather | solution.py:64
  120.5 4.3 %multiply_reduce_fusion = (f32[]{:T(128)}, f32[128,1024]{1,0:T(8,128)S(1)}) fusion(bf16[1,1024,1024]{2,1,0:T(8,128)(2,1)} %all-gather.6.cloned.1.call-done, bf16[1024,1,1024]{2,0,1:T(8,128)(2,1)} %all-gather.4.cloned.1.call-done, bf16[1,128,1024]{2,1,0:T(8,128)(2,1)S(1)} %copy-done), kind=kOutput, calls=%fused_computation.18 | convolution fusion | flops 537264128 | bytes 4980740 | tf_op jit(solution)/shard_map/rjc,jck->rjk/dot_general | solution.py:77
  124.8 17.1 %psum.7 = f32[1]{0:T(128)} all-reduce(f32[1]{0:T(128)} %bitcast.17), channel_id=1, replica_groups=mesh['fsdp_0'=4,'fsdp_1'=8,'fsdp_2'=2,'dp'=8] {'dp'}, use_global_device_ids=true, to_apply=%region_4.5 | all-reduce | flops 1 | bytes 8 | tf_op jit(solution)/shard_map/psum | solution.py:80
  142.6 0.7 fusion.28
  143.4 41.8 %all-gather.8.cloned.1.call-done = bf16[1024,1,1024]{2,0,1:T(8,128)(2,1)} async-done(((bf16[128,1,1024]{2,0,1:T(8,128)(2,1)}), bf16[1024,1,1024]{2,0,1:T(8,128)(2,1)}) %all-gather.8.cloned.1.call-update) | async-done | bytes 2097168 | tf_op jit(solution)/shard_map/all_gather | solution.py:83
  185.1 1.8 copy.30
  186.9 5.4 %all_to_all.34 = bf16[32,2,16,1,1024]{4,2,0,3,1:T(8,128)(2,1)S(1)} all-to-all(bf16[32,2,16,1,1024]{4,2,0,3,1:T(8,128)(2,1)S(1)} %copy.30), channel_id=1, replica_groups=mesh['fsdp_0'=4,'fsdp_1'=8,'fsdp_2'=2,'dp'=8] {'fsdp_2'}, dimensions={1} | all-to-all | bytes 4194304 | tf_op jit(solution)/shard_map/all_to_all | solution.py:33
  192.3 1.5 copy.31
  193.8 10.1 %all-to-all-start.3 = ((bf16[32,2,16,1,1024]{4,2,1,3,0:T(8,128)(2,1)}), bf16[32,2,16,1,1024]{4,2,1,3,0:T(8,128)(2,1)}, u32[]{:S(2)}, u32[]{:S(2)}) async-start(bf16[32,2,16,1,1024]{4,2,1,3,0:T(8,128)(2,1)} %copy.31), calls=%async_computation.3 | async-start | bytes 4194304 | tf_op jit(solution)/shard_map/all_to_all | solution.py:33
  204.0 0.1 broadcast_in_dim.61
  204.1 0.1 broadcast_in_dim.62
  204.2 1.3 fusion.14
  205.5 1.6 fusion.17
  207.1 47.3 %all-to-all-done.3 = bf16[32,2,16,1,1024]{4,2,1,3,0:T(8,128)(2,1)} async-done(((bf16[32,2,16,1,1024]{4,2,1,3,0:T(8,128)(2,1)}), bf16[32,2,16,1,1024]{4,2,1,3,0:T(8,128)(2,1)}, u32[]{:S(2)}, u32[]{:S(2)}) %all-to-all-start.3) | async-done | bytes 2097184 | tf_op jit(solution)/shard_map/all_to_all | solution.py:33
  254.4 2.2 gather_fusion.1
  256.6 0.1 copy.34
  256.6 1.1 broadcast_select_fusion
  (18 shorter events, 0.1 us)
Async XLA Ops:
  7.2 113.3 %copy-start = (bf16[1,128,1024]{2,1,0:T(8,128)(2,1)S(1)}, bf16[1,128,1024]{2,1,0:T(8,128)(2,1)}, u32[]{:S(2)}) copy-start(bf16[1,128,1024]{2,1,0:T(8,128)(2,1)} %param.10) | copy-start | bytes 786436
  7.2 69.5 %all-gather.6.cloned.1.call-start = ((), (), s32[]{:S(2)}) async-start(), calls=%async_computation.5 | async-start | bytes 2359296 | tf_op jit(solution)/shard_map/all_gather | solution.py:66
  9.2 11.7 %copy-start.4 = (s32[28]{0:T(128)S(1)}, s32[28]{0:T(128)}, u32[]{:S(2)}) copy-start(s32[28]{0:T(128)} %param.7) | copy-start | bytes 340
  10.5 43.0 %all-to-all-start = ((bf16[8,16,28,128]{3,1,2,0:T(8,128)(2,1)}), bf16[8,16,28,128]{3,1,2,0:T(8,128)(2,1)S(1)}, u32[]{:S(2)}, u32[]{:S(2)}) async-start(bf16[8,16,28,128]{3,1,2,0:T(8,128)(2,1)} %copy.27), calls=%async_computation | async-start | bytes 1835008 | tf_op jit(solution)/shard_map/all_to_all | solution.py:19
  20.8 99.7 %all-gather.4.cloned.1.call-start = ((), (), s32[]{:S(2)}) async-start(), calls=%async_computation.4 | async-start | bytes 2359296 | tf_op jit(solution)/shard_map/all_gather | solution.py:64
  76.6 108.5 %all-gather.8.cloned.1.call-start = ((), (), s32[]{:S(2)}) async-start(), calls=%async_computation.6 | async-start | bytes 2359296 | tf_op jit(solution)/shard_map/all_gather | solution.py:83
  193.8 10.4 %copy-start.1 = (bf16[1024,1,1024]{2,0,1:T(8,128)(2,1)S(1)}, bf16[1024,1,1024]{2,0,1:T(8,128)(2,1)}, u32[]{:S(2)}) copy-start(bf16[1024,1,1024]{2,0,1:T(8,128)(2,1)} %all-gather.4.cloned.1.call-done) | copy-start | bytes 6291460
  193.8 10.4 %copy-start.2 = (f32[1,128,1024]{2,1,0:T(8,128)S(1)}, f32[1,128,1024]{2,1,0:T(8,128)}, u32[]{:S(2)}) copy-start(f32[1,128,1024]{2,1,0:T(8,128)} %param.9) | copy-start | bytes 1572868
  193.8 60.5 %all-to-all-start.3 = ((bf16[32,2,16,1,1024]{4,2,1,3,0:T(8,128)(2,1)}), bf16[32,2,16,1,1024]{4,2,1,3,0:T(8,128)(2,1)}, u32[]{:S(2)}, u32[]{:S(2)}) async-start(bf16[32,2,16,1,1024]{4,2,1,3,0:T(8,128)(2,1)} %copy.31), calls=%async_computation.3 | async-start | bytes 4194304 | tf_op jit(solution)/shard_map/all_to_all | solution.py:33
  204.0 1.5 copy-start.3
Sparse Core Ops, SparseCore 0:
  10.1 58.1 all-gather.5
  76.8 43.6 all-gather.3
  143.5 41.6 all-gather.7
where the time goes:
time: 265 us; the launch traced here: 264 us
  waiting for transfers between devices  166 us (63%)
  blocking collectives  44.7 us (17%)
  starting transfers between devices  20.6 us (8%)
  between operations  14.6 us (6%)
  local copies, waits for them, and re-layouts  8.89 us (3%)
  matrix products  7.23 us (3%)
    all_to_all x1, waiting for transfers between devices, exchange_in_order(): result = lax.all_to_all(result, axes[k], k, k, tiled=True)  47.3 us
    all_gather x1, waiting for transfers between devices, per_device(): gradient = lax.all_gather(incoming, 'dp', axis=2, tiled=True)  43.8 us
    all_gather x1, waiting for transfers between devices, per_device(): full_rows = lax.all_gather(scaled, 'dp', axis=0, tiled=True)  41.8 us
    all_to_all x1, waiting for transfers between devices, sum_at_owner(): tiles = lax.all_to_all(in_blocks(array, dim, count), axis, 0, 0, tiled=True)  32.4 us
    all_to_all x1, blocking collectives, per_device(): lax.all_to_all(outgoing, FSDP, split_axis=1, concat_axis=0, tiled=True)  22.2 us
    psum x1, blocking collectives, per_device(): squares = lax.psum(jnp.sum(both_applied * both_applied, axis=(0, 2)), 'dp')  17.1 us
    all_to_all x1, starting transfers between devices, sum_at_owner(): tiles = lax.all_to_all(in_blocks(array, dim, count), axis, 0, 0, tiled=True)  10.3 us
    all_to_all x1, starting transfers between devices, exchange_in_order(): result = lax.all_to_all(result, axes[k], k, k, tiled=True)  10.1 us
  transfers between devices with their start and end apart: 5, of which 4 were waited for; matrix products, arithmetic and copies ran while one was open for 3% of the time, Pallas kernels for 0%

commit v1 on v0

--- a/solution.py
+++ b/solution.py
@@ -6,6 +6,28 @@
 
 FSDP = ("fsdp_0", "fsdp_1", "fsdp_2")
 epsilon = 1e-06
+
+
+def in_order_2(parts, dim):
+    parts = jnp.moveaxis(parts, 0, dim)
+    shape = parts.shape
+    return parts.reshape(*shape[:dim], shape[dim] * shape[dim + 1], *shape[dim + 2 :])
+
+
+def ring_gather(x, axis, dim):
+    size = lax.axis_size(axis)
+    pairs = [(i, (i + 1) % size) for i in range(size)]
+    back = [(b, a) for a, b in pairs]
+    lower, upper = ([], [])
+    for step in range(size - 1):
+        if step % 2 == 0:
+            lower.append(lax.ppermute(lower[-1] if lower else x, axis, pairs))
+        else:
+            upper.append(lax.ppermute(upper[-1] if upper else x, axis, back))
+    blocks = jnp.stack([*lower[::-1], x, *upper])
+    shift = lax.axis_index(axis) - len(lower)
+    blocks = blocks[(jnp.arange(size) - shift) % size]
+    return in_order_2(blocks, dim)
 
 
 def in_blocks(array, dim, count):
@@ -61,7 +83,7 @@
         filled[None, :, None], jnp.take(shares, source, axis=1), jnp.zeros((), jnp.bfloat16)
     )
     incoming = lax.all_to_all(outgoing, FSDP, split_axis=1, concat_axis=0, tiled=True)
-    gradient = lax.all_gather(incoming, "dp", axis=2, tiled=True)
+    gradient = ring_gather(incoming, "dp", 2)
     own_rows = lax.dynamic_slice_in_dim(gradient, row_start, shared_rows, 0)
     whole_right = lax.all_gather(right_root, "dp", axis=1, tiled=True)
     left_new = left_stats + jnp.einsum(

time: 265 us -> 258 us (0.974)
  waiting for transfers between devices: 166 us -> 125 us
  starting transfers between devices: 20.6 us -> 47 us
  local copies, waits for them, and re-layouts: 8.89 us -> 17 us
    all_gather x1 -> x0, waiting for transfers between devices: 43.8 us -> none  [per_device(): gradient = lax.all_gather(incoming, 'dp', axis=2, tiled=True)]
    ppermute x0 -> x7, starting transfers between devices: none -> 26.6 us  [the longest x4 14.6 us: ring_gather(): lower.append(lax.ppermute(lower[-1] if lower else x, axis, pairs))]
    ppermute x0 -> x7, waiting for transfers between devices: none -> 14.6 us  [the longest x4 14.6 us: ring_gather(): lower.append(lax.ppermute(lower[-1] if lower else x, axis, pairs))]
    all_to_all x1, waiting for transfers between devices: 32.4 us -> 24.4 us  [sum_at_owner(): tiles = lax.all_to_all(in_blocks(array, dim, count), axis, 0, 0, tiled=True)]
    all_gather x1, waiting for transfers between devices: 41.8 us -> 37.9 us  [per_device(): full_rows = lax.all_gather(scaled, 'dp', axis=0, tiled=True)]
    unnamed x11 -> x18, local copies, waits for them, and re-layouts: 1.33 us -> 4.46 us
    transpose x0 -> x1, local copies, waits for them, and re-layouts: none -> 2.85 us  [in_order_2(): parts = jnp.moveaxis(parts, 0, dim)]
  transfers between devices with their start and end apart: 5 -> 11, of which waited for: 4 -> 7; matrix products, arithmetic and copies ran while one was open for 3% -> 5% of each run, Pallas kernels for 0% -> 0%
where the time goes in v1:
time: 258 us; the launch traced here: 257 us
  waiting for transfers between devices  125 us (48%)
  starting transfers between devices  47 us (18%)
  blocking collectives  44 us (17%)
  local copies, waits for them, and re-layouts  17 us (7%)
  between operations  15 us (6%)
  matrix products  6.57 us (3%)
    all_to_all x1, waiting for transfers between devices, exchange_in_order(): result = lax.all_to_all(result, axes[k], k, k, tiled=True)  47.3 us
    all_gather x1, waiting for transfers between devices, per_device(): full_rows = lax.all_gather(scaled, 'dp', axis=0, tiled=True)  37.9 us
    all_to_all x1, waiting for transfers between devices, sum_at_owner(): tiles = lax.all_to_all(in_blocks(array, dim, count), axis, 0, 0, tiled=True)  24.4 us
    all_to_all x1, blocking collectives, per_device(): lax.all_to_all(outgoing, FSDP, split_axis=1, concat_axis=0, tiled=True)  21.6 us
    psum x1, blocking collectives, per_device(): squares = lax.psum(jnp.sum(both_applied * both_applied, axis=(0, 2)), 'dp')  16.9 us
    ppermute x4, starting transfers between devices, ring_gather(): lower.append(lax.ppermute(lower[-1] if lower else x, axis, pairs))  14.6 us
    ppermute x4, waiting for transfers between devices, ring_gather(): lower.append(lax.ppermute(lower[-1] if lower else x, axis, pairs))  14.6 us
    ppermute x3, starting transfers between devices, ring_gather(): upper.append(lax.ppermute(upper[-1] if upper else x, axis, back))  12 us
  transfers between devices with their start and end apart: 11, of which 7 were waited for; matrix products, arithmetic and copies ran while one was open for 5% of the time, Pallas kernels for 0%

profile of v1, /device:TPU:16, one launch (start us, length us, event | category | flops | bytes accessed | tf_op | source)
XLA Modules:
  0.0 256.9 jit_solution(9030065843454904279)
XLA Ops:
  7.2 1.3 copy.93
  8.5 1.3 copy.74
  9.8 10.3 %all-to-all-start = ((bf16[8,16,28,128]{3,1,2,0:T(8,128)(2,1)}), bf16[8,16,28,128]{3,1,2,0:T(8,128)(2,1)S(1)}, u32[]{:S(2)}, u32[]{:S(2)}) async-start(bf16[8,16,28,128]{3,1,2,0:T(8,128)(2,1)} %copy.74), calls=%async_computation | async-start | bytes 1835008 | tf_op jit(solution)/shard_map/all_to_all | solution.py:41
  21.1 24.4 %all-to-all-done = bf16[8,16,28,128]{3,1,2,0:T(8,128)(2,1)S(1)} async-done(((bf16[8,16,28,128]{3,1,2,0:T(8,128)(2,1)}), bf16[8,16,28,128]{3,1,2,0:T(8,128)(2,1)S(1)}, u32[]{:S(2)}, u32[]{:S(2)}) %all-to-all-start) | async-done | bytes 917536 | tf_op jit(solution)/shard_map/all_to_all | solution.py:41
  46.5 21.6 %all_to_all.33 = bf16[16,64,128]{2,0,1:T(8,128)(2,1)S(1)} all-to-all(bf16[16,64,128]{2,0,1:T(8,128)(2,1)S(1)} %select_bitcast_fusion), channel_id=1, replica_groups=mesh['fsdp_0'=4,'fsdp_1'=8,'fsdp_2'=2,'dp'=8] {'fsdp_0','fsdp_1','fsdp_2'}, dimensions={1} | all-to-all | bytes 524288 | tf_op jit(solution)/shard_map/all_to_all | solution.py:85
  68.1 5.4 %collective-permute-start = (bf16[1024,1,128]{2,0,1:T(8,128)(2,1)S(1)}, bf16[1024,1,128]{2,0,1:T(8,128)(2,1)S(1)}, u32[]{:S(2)}, u32[]{:S(2)}) collective-permute-start(bf16[1024,1,128]{2,0,1:T(8,128)(2,1)S(1)} %bitcast.123), channel_id=1, source_target_pairs={{0,1},{1,2},{2,3},{3,4},{4,5},{5,6},{6,7},{7,0},{8,9},{9,10},{10,1... | collective-permute-start | bytes 786440 | tf_op jit(solution)/shard_map/ppermute | solution.py:24
  73.6 6.0 %collective-permute-done = bf16[1024,1,128]{2,0,1:T(8,128)(2,1)S(1)} collective-permute-done((bf16[1024,1,128]{2,0,1:T(8,128)(2,1)S(1)}, bf16[1024,1,128]{2,0,1:T(8,128)(2,1)S(1)}, u32[]{:S(2)}, u32[]{:S(2)}) %collective-permute-start) | collective-permute-done | bytes 262176 | tf_op jit(solution)/shard_map/ppermute | solution.py:24
  79.5 4.2 %collective-permute-start.1 = (bf16[1024,1,128]{2,0,1:T(8,128)(2,1)S(1)}, bf16[1024,1,128]{2,0,1:T(8,128)(2,1)S(1)}, u32[]{:S(2)}, u32[]{:S(2)}) collective-permute-start(bf16[1024,1,128]{2,0,1:T(8,128)(2,1)S(1)} %collective-permute-done), channel_id=1, source_target_pairs={{0,1},{1,2},{2,3},{3,4},{4,5},{5,6},{6,7},{7,0},{8,9},{9,10},{10,1... | collective-permute-start | bytes 786440 | tf_op jit(solution)/shard_map/ppermute | solution.py:24
  83.8 2.8 %collective-permute-start.4 = (bf16[1024,1,128]{2,0,1:T(8,128)(2,1)S(1)}, bf16[1024,1,128]{2,0,1:T(8,128)(2,1)S(1)}, u32[]{:S(2)}, u32[]{:S(2)}) collective-permute-start(bf16[1024,1,128]{2,0,1:T(8,128)(2,1)S(1)} %bitcast.124), channel_id=1, source_target_pairs={{1,0},{2,1},{3,2},{4,3},{5,4},{6,5},{7,6},{0,7},{9,8},{10,9},{11,1... | collective-permute-start | bytes 786440 | tf_op jit(solution)/shard_map/ppermute | solution.py:26
  86.6 3.5 %collective-permute-done.1 = bf16[1024,1,128]{2,0,1:T(8,128)(2,1)S(1)} collective-permute-done((bf16[1024,1,128]{2,0,1:T(8,128)(2,1)S(1)}, bf16[1024,1,128]{2,0,1:T(8,128)(2,1)S(1)}, u32[]{:S(2)}, u32[]{:S(2)}) %collective-permute-start.1) | collective-permute-done | bytes 262176 | tf_op jit(solution)/shard_map/ppermute | solution.py:24
  90.1 3.0 %collective-permute-start.2 = (bf16[1024,1,128]{2,0,1:T(8,128)(2,1)S(1)}, bf16[1024,1,128]{2,0,1:T(8,128)(2,1)S(1)}, u32[]{:S(2)}, u32[]{:S(2)}) collective-permute-start(bf16[1024,1,128]{2,0,1:T(8,128)(2,1)S(1)} %collective-permute-done.1), channel_id=1, source_target_pairs={{0,1},{1,2},{2,3},{3,4},{4,5},{5,6},{6,7},{7,0},{8,9},{9,10},{10,1... | collective-permute-start | bytes 786440 | tf_op jit(solution)/shard_map/ppermute | solution.py:24
  93.1 4.0 %collective-permute-start.5 = (bf16[1024,1,128]{2,0,1:T(8,128)(2,1)S(1)}, bf16[1024,1,128]{2,0,1:T(8,128)(2,1)}, u32[]{:S(2)}, u32[]{:S(2)}) collective-permute-start(bf16[1024,1,128]{2,0,1:T(8,128)(2,1)S(1)} %collective-permute-done.4), channel_id=1, source_target_pairs={{1,0},{2,1},{3,2},{4,3},{5,4},{6,5},{7,6},{0,7},{9,8},{10,9},{11,1... | collective-permute-start | bytes 786440 | tf_op jit(solution)/shard_map/ppermute | solution.py:26
  97.2 2.6 %collective-permute-done.2 = bf16[1024,1,128]{2,0,1:T(8,128)(2,1)S(1)} collective-permute-done((bf16[1024,1,128]{2,0,1:T(8,128)(2,1)S(1)}, bf16[1024,1,128]{2,0,1:T(8,128)(2,1)S(1)}, u32[]{:S(2)}, u32[]{:S(2)}) %collective-permute-start.2) | collective-permute-done | bytes 262176 | tf_op jit(solution)/shard_map/ppermute | solution.py:24
  99.8 1.9 collective-permute-start.3
  101.8 5.1 %collective-permute-start.6 = (bf16[1024,1,128]{2,0,1:T(8,128)(2,1)}, bf16[1024,1,128]{2,0,1:T(8,128)(2,1)S(1)}, u32[]{:S(2)}, u32[]{:S(2)}) collective-permute-start(bf16[1024,1,128]{2,0,1:T(8,128)(2,1)} %collective-permute-done.5), channel_id=1, source_target_pairs={{1,0},{2,1},{3,2},{4,3},{5,4},{6,5},{7,6},{0,7},{9,8},{10,9},{11,1... | collective-permute-start | bytes 786440 | tf_op jit(solution)/shard_map/ppermute | solution.py:26
  106.9 2.5 collective-permute-done.3
  110.4 1.0 bitcast_dynamic-update-slice_fusion.4
  111.5 1.0 bitcast_dynamic-update-slice_fusion
  112.6 2.1 gather_fusion.1
  114.7 2.9 %copy.84 = bf16[1024,1,8,128]{0,3,2,1:T(8,128)(2,1)S(1)} copy(bf16[1024,1,8,128]{3,0,2,1:T(8,128)(2,1)} %bitcast.117) | data formatting | bytes 4194304 | tf_op jit(solution)/shard_map/transpose | solution.py:12
  117.6 3.7 %multiply_reduce_fusion = (f32[]{:T(128)}, f32[128,1024]{1,0:T(8,128)S(1)}) fusion(bf16[1,1024,1024]{2,1,0:T(8,128)(2,1)} %all-gather.3.cloned.1.call-done, bf16[1024,1024]{0,1:T(8,128)(2,1)S(1)} %bitcast.112, bf16[1,128,1024]{2,1,0:T(8,128)(2,1)S(1)} %copy-done), kind=kOutput, calls=%fused_computation.13 | convolution fusion | flops 537264128 | bytes 4980740 | tf_op jit(solution)/shard_map/rjc,jck->rjk/dot_general | solution.py:99
  121.2 16.9 %psum.7 = f32[1]{0:T(128)} all-reduce(f32[1]{0:T(128)} %bitcast.40), channel_id=1, replica_groups=mesh['fsdp_0'=4,'fsdp_1'=8,'fsdp_2'=2,'dp'=8] {'dp'}, use_global_device_ids=true, to_apply=%region_4.5 | all-reduce | flops 1 | bytes 8 | tf_op jit(solution)/shard_map/psum | solution.py:102
  139.6 37.9 %all-gather.5.cloned.1.call-done = bf16[1024,1,1024]{2,0,1:T(8,128)(2,1)} async-done(((bf16[128,1,1024]{2,0,1:T(8,128)(2,1)}), bf16[1024,1,1024]{2,0,1:T(8,128)(2,1)}) %all-gather.5.cloned.1.call-update) | async-done | bytes 2097168 | tf_op jit(solution)/shard_map/all_gather | solution.py:105
  177.6 1.8 copy.88
  179.3 5.4 %all_to_all.34 = bf16[32,2,16,1,1024]{4,2,0,3,1:T(8,128)(2,1)S(1)} all-to-all(bf16[32,2,16,1,1024]{4,2,0,3,1:T(8,128)(2,1)S(1)} %copy.88), channel_id=1, replica_groups=mesh['fsdp_0'=4,'fsdp_1'=8,'fsdp_2'=2,'dp'=8] {'fsdp_2'}, dimensions={1} | all-to-all | bytes 4194304 | tf_op jit(solution)/shard_map/all_to_all | solution.py:55
  184.8 1.5 copy.89
  186.2 10.0 %all-to-all-start.3 = ((bf16[32,2,16,1,1024]{4,2,1,3,0:T(8,128)(2,1)}), bf16[32,2,16,1,1024]{4,2,1,3,0:T(8,128)(2,1)}, u32[]{:S(2)}, u32[]{:S(2)}) async-start(bf16[32,2,16,1,1024]{4,2,1,3,0:T(8,128)(2,1)} %copy.89), calls=%async_computation.3 | async-start | bytes 4194304 | tf_op jit(solution)/shard_map/all_to_all | solution.py:55
  196.5 1.6 fusion.3
  198.1 1.3 fusion.2
  199.4 47.3 %all-to-all-done.3 = bf16[32,2,16,1,1024]{4,2,1,3,0:T(8,128)(2,1)} async-done(((bf16[32,2,16,1,1024]{4,2,1,3,0:T(8,128)(2,1)}), bf16[32,2,16,1,1024]{4,2,1,3,0:T(8,128)(2,1)}, u32[]{:S(2)}, u32[]{:S(2)}) %all-to-all-start.3) | async-done | bytes 2097184 | tf_op jit(solution)/shard_map/all_to_all | solution.py:55
  246.6 2.2 gather_fusion.2
  248.9 1.1 broadcast_select_fusion
  (41 shorter events, 4.1 us)
Async XLA Ops:
  7.2 110.4 %copy-start = (bf16[1,128,1024]{2,1,0:T(8,128)(2,1)S(1)}, bf16[1,128,1024]{2,1,0:T(8,128)(2,1)}, u32[]{:S(2)}) copy-start(bf16[1,128,1024]{2,1,0:T(8,128)(2,1)} %param.10) | copy-start | bytes 786436
  8.5 12.4 %copy-start.4 = (s32[28]{0:T(128)S(1)}, s32[28]{0:T(128)}, u32[]{:S(2)}) copy-start(s32[28]{0:T(128)} %param.7) | copy-start | bytes 340
  9.8 35.7 %all-to-all-start = ((bf16[8,16,28,128]{3,1,2,0:T(8,128)(2,1)}), bf16[8,16,28,128]{3,1,2,0:T(8,128)(2,1)S(1)}, u32[]{:S(2)}, u32[]{:S(2)}) async-start(bf16[8,16,28,128]{3,1,2,0:T(8,128)(2,1)} %copy.74), calls=%async_computation | async-start | bytes 1835008 | tf_op jit(solution)/shard_map/all_to_all | solution.py:41
  20.1 97.4 %all-gather.3.cloned.1.call-start = ((), (), s32[]{:S(2)}) async-start(), calls=%async_computation.4 | async-start | bytes 2359296 | tf_op jit(solution)/shard_map/all_gather | solution.py:88
  20.9 156.7 %all-gather.5.cloned.1.call-start = ((), (), s32[]{:S(2)}) async-start(), calls=%async_computation.5 | async-start | bytes 2359296 | tf_op jit(solution)/shard_map/all_gather | solution.py:105
  68.1 11.4 %collective-permute-start = (bf16[1024,1,128]{2,0,1:T(8,128)(2,1)S(1)}, bf16[1024,1,128]{2,0,1:T(8,128)(2,1)S(1)}, u32[]{:S(2)}, u32[]{:S(2)}) collective-permute-start(bf16[1024,1,128]{2,0,1:T(8,128)(2,1)S(1)} %bitcast.123), channel_id=1, source_target_pairs={{0,1},{1,2},{2,3},{3,4},{4,5},{5,6},{6,7},{7,0},{8,9},{9,10},{10,1... | collective-permute-start | bytes 786440 | tf_op jit(solution)/shard_map/ppermute | solution.py:24
  79.5 10.6 %collective-permute-start.1 = (bf16[1024,1,128]{2,0,1:T(8,128)(2,1)S(1)}, bf16[1024,1,128]{2,0,1:T(8,128)(2,1)S(1)}, u32[]{:S(2)}, u32[]{:S(2)}) collective-permute-start(bf16[1024,1,128]{2,0,1:T(8,128)(2,1)S(1)} %collective-permute-done), channel_id=1, source_target_pairs={{0,1},{1,2},{2,3},{3,4},{4,5},{5,6},{6,7},{7,0},{8,9},{9,10},{10,1... | collective-permute-start | bytes 786440 | tf_op jit(solution)/shard_map/ppermute | solution.py:24
  83.8 9.4 %collective-permute-start.4 = (bf16[1024,1,128]{2,0,1:T(8,128)(2,1)S(1)}, bf16[1024,1,128]{2,0,1:T(8,128)(2,1)S(1)}, u32[]{:S(2)}, u32[]{:S(2)}) collective-permute-start(bf16[1024,1,128]{2,0,1:T(8,128)(2,1)S(1)} %bitcast.124), channel_id=1, source_target_pairs={{1,0},{2,1},{3,2},{4,3},{5,4},{6,5},{7,6},{0,7},{9,8},{10,9},{11,1... | collective-permute-start | bytes 786440 | tf_op jit(solution)/shard_map/ppermute | solution.py:26
  90.1 9.7 %collective-permute-start.2 = (bf16[1024,1,128]{2,0,1:T(8,128)(2,1)S(1)}, bf16[1024,1,128]{2,0,1:T(8,128)(2,1)S(1)}, u32[]{:S(2)}, u32[]{:S(2)}) collective-permute-start(bf16[1024,1,128]{2,0,1:T(8,128)(2,1)S(1)} %collective-permute-done.1), channel_id=1, source_target_pairs={{0,1},{1,2},{2,3},{3,4},{4,5},{5,6},{6,7},{7,0},{8,9},{9,10},{10,1... | collective-permute-start | bytes 786440 | tf_op jit(solution)/shard_map/ppermute | solution.py:24
  93.1 8.6 %collective-permute-start.5 = (bf16[1024,1,128]{2,0,1:T(8,128)(2,1)S(1)}, bf16[1024,1,128]{2,0,1:T(8,128)(2,1)}, u32[]{:S(2)}, u32[]{:S(2)}) collective-permute-start(bf16[1024,1,128]{2,0,1:T(8,128)(2,1)S(1)} %collective-permute-done.4), channel_id=1, source_target_pairs={{1,0},{2,1},{3,2},{4,3},{5,4},{6,5},{7,6},{0,7},{9,8},{10,9},{11,1... | collective-permute-start | bytes 786440 | tf_op jit(solution)/shard_map/ppermute | solution.py:26
  99.8 7.1 %copy-start.3 = (bf16[1024,1,128]{2,0,1:T(8,128)(2,1)}, bf16[1024,1,128]{2,0,1:T(8,128)(2,1)S(1)}, u32[]{:S(2)}) copy-start(bf16[1024,1,128]{2,0,1:T(8,128)(2,1)S(1)} %collective-permute-done.2) | copy-start | bytes 786436
  99.8 9.6 %collective-permute-start.3 = (bf16[1024,1,128]{2,0,1:T(8,128)(2,1)S(1)}, bf16[1024,1,128]{2,0,1:T(8,128)(2,1)}, u32[]{:S(2)}, u32[]{:S(2)}) collective-permute-start(bf16[1024,1,128]{2,0,1:T(8,128)(2,1)S(1)} %collective-permute-done.2), channel_id=1, source_target_pairs={{0,1},{1,2},{2,3},{3,4},{4,5},{5,6},{6,7},{7,0},{8,9},{9,10},{10,1... | collective-permute-start | bytes 786440 | tf_op jit(solution)/shard_map/ppermute | solution.py:24
  101.8 10.7 %collective-permute-start.6 = (bf16[1024,1,128]{2,0,1:T(8,128)(2,1)}, bf16[1024,1,128]{2,0,1:T(8,128)(2,1)S(1)}, u32[]{:S(2)}, u32[]{:S(2)}) collective-permute-start(bf16[1024,1,128]{2,0,1:T(8,128)(2,1)} %collective-permute-done.5), channel_id=1, source_target_pairs={{1,0},{2,1},{3,2},{4,3},{5,4},{6,5},{7,6},{0,7},{9,8},{10,9},{11,1... | collective-permute-start | bytes 786440 | tf_op jit(solution)/shard_map/ppermute | solution.py:26
  186.2 10.2 %copy-start.1 = (f32[1,128,1024]{2,1,0:T(8,128)S(1)}, f32[1,128,1024]{2,1,0:T(8,128)}, u32[]{:S(2)}) copy-start(f32[1,128,1024]{2,1,0:T(8,128)} %param.9) | copy-start | bytes 1572868
  186.2 60.4 %all-to-all-start.3 = ((bf16[32,2,16,1,1024]{4,2,1,3,0:T(8,128)(2,1)}), bf16[32,2,16,1,1024]{4,2,1,3,0:T(8,128)(2,1)}, u32[]{:S(2)}, u32[]{:S(2)}) async-start(bf16[32,2,16,1,1024]{4,2,1,3,0:T(8,128)(2,1)} %copy.89), calls=%async_computation.3 | async-start | bytes 4194304 | tf_op jit(solution)/shard_map/all_to_all | solution.py:55
  196.2 1.8 copy-start.2
Sparse Core Ops, SparseCore 0:
  23.0 47.5 all-gather.2
  139.7 37.7 all-gather.4
